TPU v7x, 512 devices: a whole 4x4x16 slice. The times are simulated.
512 devices in a mesh: row: 16 (over x, y), col: 32 (over z, core).
Axes of the slice: x: 4, y: 4, z: 16, core: 2. Of those that a mesh axis runs over, the one named last changes fastest.
Arguments:
- arrival: float32 [64, 16384], P(None, 'col'), may hold values from 0 to 4
- delay: bfloat16 [4, 16384, 16384], P(None, 'col', 'row'), may hold values from -40 to 20
- occupancy: int32 [4, 32, 32], replicated, may hold values from 0 to 1, as said below
Outputs:
- final_arrival: float32 [64, 16384], P(None, 'col')
- worst: float32 [64], replicated
Inputs may be any that keep to these rules, and one draw needn't show every extreme that they name: In every level every column of tiles holds at least one tile with occupancy 1.
All inputs are finite; a program needn't handle non-finite values.
Results may differ from a plain program's by a relative error of at most 0.0009.
Values sent between devices are 32-bit elements; how exact they have to be, the bound alone decides.
A program may use at most 64 MiB of HBM per device.

v0:
```python
import functools

import jax
import jax.numpy as jnp
from jax import lax
from jax.experimental import pallas as pl
from jax.experimental.pallas import tpu as pltpu
from jax.sharding import PartitionSpec as P

MESH = pl.DeviceIdType.MESH
LANES = 128
GROUP = 128
LAG = 3
LOW = -1000000000.0


def kernel(
    rows, cols, arrival_ref, delay_hbm, occ_ref, out_ref, worst_ref,
    delay_ref, wide_ref, part_ref, pair_ref, comb_ref, rs_ref, fin_ref, times_ref, peak_ref, top_ref,
    load_sem, pair_send, pair_recv, rs_send, rs_recv, times_send, times_recv, peak_send, peak_recv, top_send, top_recv,
):
    level_count, tile, width = delay_hbm.shape
    ratio = cols // rows
    groups, slices, ss, sp = times_ref.shape[1:]
    pin_groups = tile // sp
    sub = slices // pin_groups
    gscen = sub * ss
    row = lax.axis_index("row")
    col = lax.axis_index("col")
    z = col // ratio
    p = col % ratio

    barrier = pltpu.get_barrier_semaphore()

    def greet(to_row, to_col):
        pl.semaphore_signal(barrier, inc=1, device_id=(to_row, to_col), device_id_type=MESH)

    for n in range(1, cols):
        greet(row, lax.rem(col + n, cols))
    for n in range(1, rows):
        greet(lax.rem(row + n, rows), col)
        greet(lax.rem(row + n, rows), row * ratio + p)
        greet(z, lax.rem(z + n, slices) * ratio + p)

    @pl.when(row != z)
    def _():
        greet(row, row * ratio + p)
        greet(z, z * ratio + p)

    peers = cols - 1 + 3 * (rows - 1) + 2 * (row != z).astype(jnp.int32)

    def load(level):
        return pltpu.make_async_copy(delay_hbm.at[level], delay_ref.at[level], load_sem.at[level])

    for level in range(level_count):
        load(level).start()

    def widen(level):
        def step(i, carry):
            at = pl.ds(pl.multiple_of(i * 64, 64), 64)
            wide_ref[level, pl.ds(i * 8, 8)] = delay_ref[level, at, :].astype(jnp.float32).reshape(8, 8, width)
            return carry

        lax.fori_loop(0, tile // 64, step, 0)

    for h in range(groups):
        for g in range(sub):
            for k in range(pin_groups):
                start = h * gscen + g * ss
                times_ref[0, h, g * pin_groups + k] = arrival_ref[start:start + ss, k * sp:(k + 1) * sp]
    load(0).wait()
    widen(0)

    def compute(level, h, middle):
        def step(n, best):
            @pl.when(n == tile // GROUP // 2)
            def _():
                middle()

            k = n // (sp // GROUP)
            value = jnp.concatenate([times_ref[level, h, g * pin_groups + k] for g in range(sub)], axis=0)
            if GROUP < sp:
                value = pltpu.roll(value, sp - (n % (sp // GROUP)) * GROUP, 1)
            for i in range(GROUP):
                spread = jnp.broadcast_to(value[:, i:i + 1], (gscen, LANES))
                best = tuple(jnp.maximum(b, spread + wide_ref[level, n * (GROUP // 8) + i // 8, i % 8:i % 8 + 1, c * LANES:(c + 1) * LANES]) for c, b in enumerate(best))
            return best

        best = lax.fori_loop(0, tile // GROUP, step, (jnp.full((gscen, LANES), LOW, jnp.float32),) * (width // LANES))
        best = jnp.concatenate(best, axis=1)
        for q in range(ratio):
            flag = occ_ref[level, col, row * ratio + q]
            for g in range(sub):
                for k in range(pin_groups):
                    start = q * tile + k * sp
                    piece = best[g * ss:(g + 1) * ss, start:start + sp]
                    part_ref[level, q, h, g * pin_groups + k] = jnp.where(flag > 0, piece, jnp.float32(LOW))

    def pair_copy(level, h, q, slot):
        return pltpu.make_async_remote_copy(
            src_ref=part_ref.at[level, q, h], dst_ref=pair_ref.at[level, slot, h],
            send_sem=pair_send.at[level, h, q], recv_sem=pair_recv.at[level, h, slot],
            device_id=(row, z * ratio + q), device_id_type=MESH)

    def rs_copy(level, h, other, slot):
        return pltpu.make_async_remote_copy(
            src_ref=comb_ref.at[level, h, other], dst_ref=rs_ref.at[level, h, slot],
            send_sem=rs_send.at[level, h, other], recv_sem=rs_recv.at[level, h, slot],
            device_id=(row, other * ratio + p), device_id_type=MESH)

    def times_copy(level, h, to, slot):
        return pltpu.make_async_remote_copy(
            src_ref=fin_ref.at[level, h], dst_ref=times_ref.at[level + 1, h, slot],
            send_sem=times_send.at[level, h, to], recv_sem=times_recv.at[level, h, slot],
            device_id=(to, row * ratio + p), device_id_type=MESH)

    def wait_times(level, h):
        for n in range(1, slices):
            times_copy(level, h, 0, lax.rem(z + n, slices)).wait_recv()

        @pl.when(row != z)
        def _():
            times_copy(level, h, 0, z).wait_recv()

    def combine(level, h):
        total = part_ref[level, p, h]
        for n in range(1, ratio):
            q = lax.rem(p + n, ratio)
            pair_copy(level, h, q, q).wait_recv()
            total = jnp.maximum(total, pair_ref[level, q, h])
        comb_ref[level, h] = total
        for n in range(1, slices):
            rs_copy(level, h, lax.rem(z + n, slices), z).start()

    def finish(level, h):
        total = comb_ref[level, h, z]
        for n in range(1, slices):
            other = lax.rem(z + n, slices)
            rs_copy(level, h, other, other).wait_recv()
            total = jnp.maximum(total, rs_ref[level, h, other])
        fin_ref[level, h] = total
        for n in range(1, rows):
            times_copy(level, h, lax.rem(row + n, rows), z).start()

        @pl.when(row != z)
        def _():
            times_copy(level, h, row, z).start()

        @pl.when(row == z)
        def _():
            times_ref[level + 1, h, z] = fin_ref[level, h]

    def one_level(level, carry):
        for h in range(groups):
            @pl.when(level > 0)
            def _():
                wait_times(level - 1, h)

            def middle():
                if h >= 1:
                    combine(level, h - 1)
                else:
                    @pl.when(level > 0)
                    def _():
                        finish(level - 1, groups - 1)
                if h >= LAG:
                    finish(level, h - LAG)

            compute(level, h, middle)
            for n in range(1, ratio):
                pair_copy(level, h, lax.rem(p + n, ratio), p).start()

        @pl.when(level + 1 < level_count)
        def _():
            load(level + 1).wait()
            widen(level + 1)

        combine(level, groups - 1)
        for h in range(max(0, groups - LAG), groups - 1):
            finish(level, h)
        return carry

    pl.semaphore_wait(barrier, peers)
    lax.fori_loop(0, level_count, one_level, 0)
    finish(level_count - 1, groups - 1)

    lane = lax.broadcasted_iota(jnp.int32, (ss, LANES), 1)
    line = lax.broadcasted_iota(jnp.int32, (ss, LANES), 0)
    peak = jnp.full((1, LANES), LOW, jnp.float32)
    for h in range(groups):
        top = jnp.max(fin_ref[level_count - 1, h], axis=1, keepdims=True)
        shown = jnp.where(lane == line + h * gscen + z // pin_groups * ss, top, jnp.float32(LOW))
        peak = jnp.maximum(peak, jnp.max(shown, axis=0, keepdims=True))
    peak_ref[col] = peak

    def peak_copy(other, slot):
        return pltpu.make_async_remote_copy(
            src_ref=peak_ref.at[col], dst_ref=peak_ref.at[slot],
            send_sem=peak_send.at[other], recv_sem=peak_recv.at[slot],
            device_id=(row, other), device_id_type=MESH)

    def top_copy(other, slot):
        return pltpu.make_async_remote_copy(
            src_ref=top_ref.at[row], dst_ref=top_ref.at[slot],
            send_sem=top_send.at[other], recv_sem=top_recv.at[slot],
            device_id=(other, col), device_id_type=MESH)

    for n in range(1, cols):
        peak_copy(lax.rem(col + n, cols), col).start()
    for n in range(1, cols):
        other = lax.rem(col + n, cols)
        peak_copy(other, other).wait_recv()
        peak = jnp.maximum(peak, peak_ref[other])
    top_ref[row] = peak
    for n in range(1, rows):
        top_copy(lax.rem(row + n, rows), row).start()

    for h in range(groups):
        wait_times(level_count - 1, h)
        for g in range(sub):
            for k in range(pin_groups):
                start = h * gscen + g * ss
                out_ref[start:start + ss, k * sp:(k + 1) * sp] = times_ref[level_count, h, g * pin_groups + k]

    def settle(level, carry):
        for h in range(groups):
            for n in range(1, ratio):
                pair_copy(level, h, lax.rem(p + n, ratio), p).wait_send()
            for n in range(1, slices):
                rs_copy(level, h, lax.rem(z + n, slices), z).wait_send()
            for n in range(1, rows):
                times_copy(level, h, lax.rem(row + n, rows), z).wait_send()

            @pl.when(row != z)
            def _():
                times_copy(level, h, row, z).wait_send()

        return carry

    lax.fori_loop(0, level_count, settle, 0)

    for n in range(1, rows):
        other = lax.rem(row + n, rows)
        top_copy(other, other).wait_recv()
        peak = jnp.maximum(peak, top_ref[other])
    worst_ref[...] = peak
    for n in range(1, cols):
        peak_copy(lax.rem(col + n, cols), col).wait_send()
    for n in range(1, rows):
        top_copy(lax.rem(row + n, rows), row).wait_send()


def shards(arrival, delay, occupancy):
    rows, cols = lax.axis_size("row"), lax.axis_size("col")
    scenarios, tile = arrival.shape
    level_count, _, width = delay.shape
    ratio = cols // rows
    sp = LANES
    pin_groups = tile // sp
    sub = rows // pin_groups
    ss = max(8, 16 // sub)
    groups = scenarios // (sub * ss)
    vmem = pl.BlockSpec(memory_space=pltpu.VMEM)
    f32 = jnp.float32
    dma = pltpu.SemaphoreType.DMA
    times, worst = pl.pallas_call(
        functools.partial(kernel, rows, cols),
        out_shape=(
            jax.ShapeDtypeStruct((scenarios, tile), f32),
            jax.ShapeDtypeStruct((1, LANES), f32),
        ),
        in_specs=[vmem, pl.BlockSpec(memory_space=pltpu.HBM), pl.BlockSpec(memory_space=pltpu.SMEM)],
        out_specs=(vmem, vmem),
        scratch_shapes=[
            pltpu.VMEM((level_count, tile, width), delay.dtype),
            pltpu.VMEM((level_count, tile // 8, 8, width), f32),
            pltpu.VMEM((level_count, ratio, groups, rows, ss, sp), f32),
            pltpu.VMEM((level_count, ratio, groups, rows, ss, sp), f32),
            pltpu.VMEM((level_count, groups, rows, ss, sp), f32),
            pltpu.VMEM((level_count, groups, rows, ss, sp), f32),
            pltpu.VMEM((level_count, groups, ss, sp), f32),
            pltpu.VMEM((level_count + 1, groups, rows, ss, sp), f32),
            pltpu.VMEM((cols, 1, LANES), f32),
            pltpu.VMEM((rows, 1, LANES), f32),
            dma((level_count,)),
            dma((level_count, groups, ratio)), dma((level_count, groups, ratio)),
            dma((level_count, groups, rows)), dma((level_count, groups, rows)),
            dma((level_count, groups, rows)), dma((level_count, groups, rows)),
            dma((cols,)), dma((cols,)),
            dma((rows,)), dma((rows,)),
        ],
        compiler_params=pltpu.CompilerParams(collective_id=0, has_side_effects=True, vmem_limit_bytes=60 * 1024 * 1024),
    )(arrival, delay, occupancy)
    return times, worst[0, :scenarios]


def solution(mesh):
    placed = (P(None, "col"), P(None, "col", "row"), P())
    return jax.shard_map(
        shards, mesh=mesh, in_specs=placed, out_specs=(P(None, "col"), P()), check_vma=False
    )
```

profile of v0, /device:TPU:1, one launch (start us, length us, event | category | flops | bytes accessed | tf_op | source)
XLA Modules:
  0.0 198.3 jit_solution(3040268414936527196)
XLA Ops:
  0.6 194.9 %shard_map.50 = (f32[64,512]{1,0:T(8,128)}, f32[1,128]{1,0:T(1,128)}) custom-call(f32[64,512]{1,0:T(8,128)} %arrival_ref.1, bf16[4,512,1024]{2,1,0:T(8,128)(2,1)} %delay_hbm.1, s32[4,32,32]{2,1,0:T(8,128)} %occ_ref.1), custom_call_target="tpu_custom_call" | custom-call | tf_op jit(solution)/shard_map/pallas_call | solution.py:266
  195.6 1.2 slice_bitcast_fusion
  196.7 1.6 copy.6
where the time goes:
time: 199 us; the launch traced here: 198 us
  Pallas kernels  195 us (98%)
  local copies, waits for them, and re-layouts  2.74 us (1%)
    pallas_call x1, Pallas kernels, shards(): pl.pallas_call(functools.partial(kernel, rows, cols), out_shape=(jax.Shap...  195 us

commit v1 on v0

v1 whole, which is shorter than its diff:
```python
import functools

import jax
import jax.numpy as jnp
from jax import lax
from jax.experimental import pallas as pl
from jax.experimental.pallas import tpu as pltpu
from jax.sharding import PartitionSpec as P

MESH = pl.DeviceIdType.MESH
LANES = 128
GROUPS = 4
LOW = -1000000000.0


def kernel(
    rows, cols, arrival_ref, delay_hbm, occ_ref, out_ref, worst_ref,
    delay_ref, wide_ref, times_ref, part_ref, near_ref, comb_ref, far_ref, fin_ref, crest_ref, peak_ref, top_ref,
    load_sem, near_send, near_recv, far_send, far_recv, times_send, times_recv, peak_send, peak_recv, top_send, top_recv,
):
    level_count, tile, width = delay_hbm.shape
    groups, side, gscen, sp = times_ref.shape[1:]
    ratio = cols // rows
    row = lax.axis_index("row")
    col = lax.axis_index("col")
    x = row // side
    y = row % side
    z = col // ratio
    p = col % ratio
    keeper = z % side == y
    last = level_count - 1

    def turn(value, n, size):
        return lax.rem(value + n, size)

    barrier = pltpu.get_barrier_semaphore()

    def greet(to_row, to_col):
        pl.semaphore_signal(barrier, inc=1, device_id=(to_row, to_col), device_id_type=MESH)

    for n in range(1, cols):
        greet(row, turn(col, n, cols))
    for n in range(1, rows):
        greet(turn(row, n, rows), col)
    for i in range(1, side):
        for c in range(1, ratio):
            greet(turn(x, i, side) * side + y, z * ratio + turn(p, c, ratio))
    peers = cols - 1 + rows - 1 + (side - 1) * (ratio - 1)

    def load(level):
        return pltpu.make_async_copy(delay_hbm.at[level], delay_ref.at[level], load_sem.at[level])

    for level in range(level_count):
        load(level).start()

    def widen(level):
        def step(i, carry):
            at = pl.ds(pl.multiple_of(i * 64, 64), 64)
            wide_ref[level, pl.ds(i * 8, 8)] = delay_ref[level, at, :].astype(jnp.float32).reshape(8, 8, width)
            return carry

        lax.fori_loop(0, tile // 64, step, 0)

    for g in range(groups):
        for k in range(side):
            times_ref[0, g, k] = arrival_ref[g * gscen:(g + 1) * gscen, k * sp:(k + 1) * sp]
    load(0).wait()
    widen(0)
    pl.semaphore_wait(barrier, peers)

    def near_copy(level, g, i, c):
        to_x = turn(x, i, side)
        to_p = turn(p, c, ratio)
        return pltpu.make_async_remote_copy(
            src_ref=part_ref.at[level, g, to_p * side + to_x], dst_ref=near_ref.at[level, g, i * ratio + c],
            send_sem=near_send.at[level, g], recv_sem=near_recv.at[level, g],
            device_id=(to_x * side + y, z * ratio + to_p), device_id_type=MESH)

    def near_all(level, g):
        some = near_ref.at[level, g, pl.ds(1, side * ratio - 1)]
        return pltpu.make_async_remote_copy(
            src_ref=some, dst_ref=some, send_sem=near_send.at[level, g], recv_sem=near_recv.at[level, g],
            device_id=(turn(x, 1, side) * side + y, col), device_id_type=MESH)

    def spot(i):
        return turn(x, side - i, side) * side + y

    def far_copy(level, g, i):
        return pltpu.make_async_remote_copy(
            src_ref=comb_ref.at[level, g, i], dst_ref=far_ref.at[level, g, turn(z, rows - spot(i), rows)],
            send_sem=far_send.at[level, g], recv_sem=far_recv.at[level, g],
            device_id=(row, spot(i) * ratio + p), device_id_type=MESH)

    def far_all(level, g, count):
        some = far_ref.at[level, g, pl.ds(1, count)]
        return pltpu.make_async_remote_copy(
            src_ref=some, dst_ref=some, send_sem=far_send.at[level, g], recv_sem=far_recv.at[level, g],
            device_id=(row, turn(z, 1, rows) * ratio + p), device_id_type=MESH)

    steps = sorted(
        ((a, b) for a in range(side) for b in range(side) if a or b),
        key=lambda s: -(min(s[0], side - s[0]) + min(s[1], side - s[1])))

    def times_copy(level, g, a, b, k):
        return pltpu.make_async_remote_copy(
            src_ref=fin_ref.at[level, g], dst_ref=times_ref.at[level + 1, g, k],
            send_sem=times_send.at[level, g], recv_sem=times_recv.at[level, g, k],
            device_id=(turn(x, a, side) * side + turn(y, b, side), col), device_id_type=MESH)

    def times_all(level, g):
        some = far_ref.at[level, g, pl.ds(1, rows - 1)]
        return pltpu.make_async_remote_copy(
            src_ref=some, dst_ref=some, send_sem=times_send.at[level, g], recv_sem=times_recv.at[level, g, 0],
            device_id=(turn(row, 1, rows), col), device_id_type=MESH)

    def wait_times(level, g, k):
        @pl.when(jnp.logical_not(jnp.logical_and(keeper, k == x)))
        def _():
            times_copy(level, g, 0, 1, k).wait_recv()

    def compute(level, g, hooks):
        def step(n, best):
            for at, hook in hooks:
                pl.when(n == at)(hook)
            k = turn(x, jnp.where(n < 2, n, side + 1 - n), side)

            @pl.when(level > 0)
            def _():
                wait_times(level - 1, g, k)

            value = times_ref[level, g, k]
            for i in range(sp):
                spread = jnp.broadcast_to(value[:, i:i + 1], (gscen, LANES))
                best = tuple(jnp.maximum(b, spread + wide_ref[level, k * (sp // 8) + i // 8, i % 8:i % 8 + 1, c * LANES:(c + 1) * LANES]) for c, b in enumerate(best))
            return best

        best = lax.fori_loop(0, side, step, (jnp.full((gscen, LANES), LOW, jnp.float32),) * (width // LANES))
        crest = jnp.full((gscen, LANES), LOW, jnp.float32)
        for q in range(ratio):
            flag = occ_ref[level, col, row * ratio + q]
            for k in range(side):
                piece = jnp.where(flag > 0, best[q * side + k], jnp.float32(LOW))
                part_ref[level, g, q * side + k] = piece
                crest = jnp.maximum(crest, piece)
        for i in (2, 1, 3, 0):
            for c in range(ratio):
                if i or c:
                    near_copy(level, g, i, c).start()
        crest_ref[g] = crest

    def combine(level, g):
        near_all(level, g).wait_recv()
        for i in range(side):
            total = near_ref[level, g, i * ratio] if i else part_ref[level, g, p * side + x]
            for c in range(1, ratio):
                total = jnp.maximum(total, near_ref[level, g, i * ratio + c])
            comb_ref[level, g, i] = total

            @pl.when(z != spot(i))
            def _():
                far_copy(level, g, i).start()

            @pl.when(z == spot(i))
            def _():
                far_ref[level, g, 0] = total

    def finish(level, g):
        @pl.when(keeper)
        def _():
            far_all(level, g, rows - 1).wait_recv()
            total = far_ref[level, g, 0]
            for n in range(1, rows):
                total = jnp.maximum(total, far_ref[level, g, n])
            fin_ref[level, g] = total
            for a, b in steps:
                times_copy(level, g, a, b, x).start()
            times_ref[level + 1, g, x] = total

    def settle(level):
        for g in range(groups):
            near_all(level, g).wait_send()

            @pl.when(jnp.logical_not(keeper))
            def _():
                far_all(level, g, side).wait_send()

            @pl.when(keeper)
            def _():
                far_all(level, g, side - 1).wait_send()
                times_all(level, g).wait_send()

    def peak_copy(n):
        return pltpu.make_async_remote_copy(
            src_ref=peak_ref.at[0], dst_ref=peak_ref.at[n], send_sem=peak_send.at[n], recv_sem=peak_recv.at[n],
            device_id=(row, turn(col, n, cols)), device_id_type=MESH)

    def top_copy(n):
        return pltpu.make_async_remote_copy(
            src_ref=top_ref.at[0], dst_ref=top_ref.at[n], send_sem=top_send.at[n], recv_sem=top_recv.at[n],
            device_id=(turn(row, n, rows), col), device_id_type=MESH)

    def peaks():
        lane = lax.broadcasted_iota(jnp.int32, (gscen, LANES), 1)
        line = lax.broadcasted_iota(jnp.int32, (gscen, LANES), 0)
        peak = jnp.full((1, LANES), LOW, jnp.float32)
        for g in range(groups):
            most = jnp.max(crest_ref[g], axis=1, keepdims=True)
            shown = jnp.where(lane == line + g * gscen, most, jnp.float32(LOW))
            peak = jnp.maximum(peak, jnp.max(shown, axis=0, keepdims=True))
        peak_ref[0] = peak
        for n in range(1, cols):
            peak_copy(n).start()

    def one_level(level, carry):
        @pl.when(level > 0)
        def _():
            finish(level - 1, 2)

        def late():
            @pl.when(level > 0)
            def _():
                finish(level - 1, 3)

        compute(level, 0, [(2, late)])
        compute(level, 1, [])
        compute(level, 2, [(3, lambda: combine(level, 0))])
        compute(level, 3, [(3, lambda: combine(level, 1))])

        @pl.when(level == last)
        def _():
            peaks()

        @pl.when(level < last)
        def _():
            load(level + 1).wait()
            widen(level + 1)

        combine(level, 2)

        @pl.when(level > 0)
        def _():
            settle(level - 1)

        combine(level, 3)
        finish(level, 0)
        finish(level, 1)
        return carry

    lax.fori_loop(0, level_count, one_level, 0)
    finish(last, 2)
    top = peak_ref[0]
    for n in range(1, cols):
        peak_copy(n).wait_recv()
        top = jnp.maximum(top, peak_ref[n])
    top_ref[0] = top
    for n in range(1, rows):
        top_copy(n).start()
    finish(last, 3)

    for g in range(groups):
        for k in range(side):
            wait_times(last, g, k)
            out_ref[g * gscen:(g + 1) * gscen, k * sp:(k + 1) * sp] = times_ref[level_count, g, k]
    for n in range(1, rows):
        top_copy(n).wait_recv()
        top = jnp.maximum(top, top_ref[n])
    worst_ref[...] = top
    settle(last)
    for n in range(1, cols):
        peak_copy(n).wait_send()
    for n in range(1, rows):
        top_copy(n).wait_send()


def shards(side, arrival, delay, occupancy):
    rows, cols = lax.axis_size("row"), lax.axis_size("col")
    scenarios, tile = arrival.shape
    level_count, _, width = delay.shape
    ratio = cols // rows
    sp = tile // side
    gscen = scenarios // GROUPS
    vmem = pl.BlockSpec(memory_space=pltpu.VMEM)
    f32 = jnp.float32
    dma = pltpu.SemaphoreType.DMA
    lg = (level_count, GROUPS)
    times, worst = pl.pallas_call(
        functools.partial(kernel, rows, cols),
        out_shape=(
            jax.ShapeDtypeStruct((scenarios, tile), f32),
            jax.ShapeDtypeStruct((1, LANES), f32),
        ),
        in_specs=[vmem, pl.BlockSpec(memory_space=pltpu.HBM), pl.BlockSpec(memory_space=pltpu.SMEM)],
        out_specs=(vmem, vmem),
        scratch_shapes=[
            pltpu.VMEM((level_count, tile, width), delay.dtype),
            pltpu.VMEM((level_count, tile // 8, 8, width), f32),
            pltpu.VMEM((level_count + 1, GROUPS, side, gscen, sp), f32),
            pltpu.VMEM((*lg, ratio * side, gscen, sp), f32),
            pltpu.VMEM((*lg, ratio * side, gscen, sp), f32),
            pltpu.VMEM((*lg, side, gscen, sp), f32),
            pltpu.VMEM((*lg, rows, gscen, sp), f32),
            pltpu.VMEM((*lg, gscen, sp), f32),
            pltpu.VMEM((GROUPS, gscen, LANES), f32),
            pltpu.VMEM((cols, 1, LANES), f32),
            pltpu.VMEM((rows, 1, LANES), f32),
            dma((level_count,)),
            dma(lg), dma(lg),
            dma(lg), dma(lg),
            dma(lg), dma((*lg, side)),
            dma((cols,)), dma((cols,)),
            dma((rows,)), dma((rows,)),
        ],
        compiler_params=pltpu.CompilerParams(collective_id=0, has_side_effects=True, vmem_limit_bytes=60 * 1024 * 1024),
    )(arrival, delay, occupancy)
    return times, worst[0, :scenarios]


def solution(mesh):
    side = 1
    while side * side < mesh.shape["row"]:
        side += 1
    placed = (P(None, "col"), P(None, "col", "row"), P())
    return jax.shard_map(
        functools.partial(shards, side), mesh=mesh, in_specs=placed, out_specs=(P(None, "col"), P()), check_vma=False
    )
```

time: 199 us -> 109 us (0.55)
  Pallas kernels: 195 us -> 106 us
    pallas_call x1, Pallas kernels: 195 us -> 106 us  [shards(): pl.pallas_call(functools.partial(kernel, rows, cols), out_shape=(jax.Shap...]
where the time goes in v1:
time: 109 us
  Pallas kernels  106 us (97%)
  local copies, waits for them, and re-layouts  2.74 us (3%)
    pallas_call x1, Pallas kernels, shards(): pl.pallas_call(functools.partial(kernel, rows, cols), out_shape=(jax.Shap...  106 us

profile of v1, /device:TPU:1, one launch (start us, length us, event | category | flops | bytes accessed | tf_op | source)
XLA Modules:
  0.0 109.1 jit_solution(13041041214523759548)
XLA Ops:
  0.6 105.7 %shard_map.50 = (f32[64,512]{1,0:T(8,128)}, f32[1,128]{1,0:T(1,128)}) custom-call(f32[64,512]{1,0:T(8,128)} %arrival_ref.1, bf16[4,512,1024]{2,1,0:T(8,128)(2,1)} %delay_hbm.1, s32[4,32,32]{2,1,0:T(8,128)} %occ_ref.1), custom_call_target="tpu_custom_call" | custom-call | tf_op jit(solution)/shard_map/pallas_call | solution.py:286
  106.4 1.2 %slice_bitcast_fusion = f32[64]{0:T(128)} fusion(f32[1,128]{1,0:T(1,128)} %get-tuple-element.5), kind=kLoop, calls=%fused_computation | loop fusion | bytes 512 | tf_op jit(solution)/shard_map/squeeze | solution.py:315
  107.5 1.6 %copy.6 = f32[64,512]{1,0:T(8,128)} copy(f32[64,512]{1,0:T(8,128)} %get-tuple-element.8) | data formatting | bytes 262144

commit v2 on v1

--- a/solution.py
+++ b/solution.py
@@ -9,14 +9,14 @@
 
 MESH = pl.DeviceIdType.MESH
 LANES = 128
-GROUPS = 4
+GROUPS = 8
 LOW = -1000000000.0
 
 
 def kernel(
-    rows, cols, arrival_ref, delay_hbm, occ_ref, out_ref, worst_ref,
-    delay_ref, wide_ref, times_ref, part_ref, near_ref, comb_ref, far_ref, fin_ref, crest_ref, peak_ref, top_ref,
-    load_sem, near_send, near_recv, far_send, far_recv, times_send, times_recv, peak_send, peak_recv, top_send, top_recv,
+    rows, cols, arrival_hbm, delay_hbm, occ_hbm, out_hbm, worst_ref,
+    occ_ref, delay_ref, wide_ref, times_ref, part_ref, near_ref, comb_ref, far_ref, fin_ref, crest_ref, peak_ref, top_ref,
+    start_sem, occ_sem, load_sem, out_sem, near_send, near_recv, far_send, far_recv, times_send, times_recv, peak_send, peak_recv, top_send, top_recv,
 ):
     level_count, tile, width = delay_hbm.shape
     groups, side, gscen, sp = times_ref.shape[1:]
@@ -47,39 +47,50 @@
             greet(turn(x, i, side) * side + y, z * ratio + turn(p, c, ratio))
     peers = cols - 1 + rows - 1 + (side - 1) * (ratio - 1)
 
-    def load(level):
-        return pltpu.make_async_copy(delay_hbm.at[level], delay_ref.at[level], load_sem.at[level])
-
-    for level in range(level_count):
-        load(level).start()
-
-    def widen(level):
+    def load(level, k):
+        at = pl.ds(k * sp, sp)
+        return pltpu.make_async_copy(delay_hbm.at[level, at], delay_ref.at[level, at], load_sem.at[level, k])
+
+    def arrive(k):
+        return pltpu.make_async_copy(arrival_hbm.at[:, :, pl.ds(k * sp, sp)], times_ref.at[0, :, k], start_sem.at[k])
+
+    flags = pltpu.make_async_copy(occ_hbm, occ_ref, occ_sem)
+
+    def widen(level, k):
         def step(i, carry):
-            at = pl.ds(pl.multiple_of(i * 64, 64), 64)
-            wide_ref[level, pl.ds(i * 8, 8)] = delay_ref[level, at, :].astype(jnp.float32).reshape(8, 8, width)
+            at = pl.ds(pl.multiple_of(k * sp + i * 64, 64), 64)
+            wide_ref[level, pl.ds(k * (sp // 8) + i * 8, 8)] = delay_ref[level, at, :].astype(jnp.float32).reshape(8, 8, width)
             return carry
 
-        lax.fori_loop(0, tile // 64, step, 0)
-
-    for g in range(groups):
+        lax.fori_loop(0, sp // 64, step, 0)
+
+    for k in range(side):
+        load(0, k).start()
+    for k in range(side):
+        arrive(k).start()
+    flags.start()
+    for level in range(1, level_count):
         for k in range(side):
-            times_ref[0, g, k] = arrival_ref[g * gscen:(g + 1) * gscen, k * sp:(k + 1) * sp]
-    load(0).wait()
-    widen(0)
-    pl.semaphore_wait(barrier, peers)
+            load(level, k).start()
+    for k in range(side):
+        load(0, k).wait()
+        widen(0, k)
+    for k in range(side):
+        arrive(k).wait()
+    flags.wait()
 
     def near_copy(level, g, i, c):
         to_x = turn(x, i, side)
         to_p = turn(p, c, ratio)
         return pltpu.make_async_remote_copy(
             src_ref=part_ref.at[level, g, to_p * side + to_x], dst_ref=near_ref.at[level, g, i * ratio + c],
-            send_sem=near_send.at[level, g], recv_sem=near_recv.at[level, g],
+            send_sem=near_send.at[level, g], recv_sem=near_recv.at[level, g, i],
             device_id=(to_x * side + y, z * ratio + to_p), device_id_type=MESH)
 
-    def near_all(level, g):
-        some = near_ref.at[level, g, pl.ds(1, side * ratio - 1)]
-        return pltpu.make_async_remote_copy(
-            src_ref=some, dst_ref=some, send_sem=near_send.at[level, g], recv_sem=near_recv.at[level, g],
+    def near_some(level, g, i, count):
+        some = near_ref.at[level, g, pl.ds(1, count)]
+        return pltpu.make_async_remote_copy(
+            src_ref=some, dst_ref=some, send_sem=near_send.at[level, g], recv_sem=near_recv.at[level, g, i],
             device_id=(turn(x, 1, side) * side + y, col), device_id_type=MESH)
 
     def spot(i):
@@ -118,10 +129,32 @@
         def _():
             times_copy(level, g, 0, 1, k).wait_recv()
 
-    def compute(level, g, hooks):
+    def compute(level, g):
         def step(n, best):
-            for at, hook in hooks:
-                pl.when(n == at)(hook)
+            @pl.when(jnp.logical_and(jnp.logical_and(level == 0, g == 0), n == side - 1))
+            def _():
+                pl.semaphore_wait(barrier, peers)
+
+            @pl.when(n == 0)
+            def _():
+                @pl.when(jnp.logical_and(level > 0, g == 0))
+                def _():
+                    combine(level - 1, groups - 1)
+
+                @pl.when(jnp.logical_and(level > 0, g < 3))
+                def _():
+                    finish(level - 1, g + 2)
+
+            @pl.when(n == side - 1)
+            def _():
+                @pl.when(jnp.logical_and(level > 0, jnp.logical_and(g >= 2, g <= 4)))
+                def _():
+                    finish(level - 1, g + 3)
+
+                @pl.when(g >= 3)
+                def _():
+                    combine(level, g - 3)
+
             k = turn(x, jnp.where(n < 2, n, side + 1 - n), side)
 
             @pl.when(level > 0)
@@ -142,15 +175,16 @@
                 piece = jnp.where(flag > 0, best[q * side + k], jnp.float32(LOW))
                 part_ref[level, g, q * side + k] = piece
                 crest = jnp.maximum(crest, piece)
+        crest_ref[g] = crest
+
         for i in (2, 1, 3, 0):
             for c in range(ratio):
                 if i or c:
                     near_copy(level, g, i, c).start()
-        crest_ref[g] = crest
 
     def combine(level, g):
-        near_all(level, g).wait_recv()
-        for i in range(side):
+        for i in (0, 1, 3, 2):
+            near_some(level, g, i, ratio if i else ratio - 1).wait_recv()
             total = near_ref[level, g, i * ratio] if i else part_ref[level, g, p * side + x]
             for c in range(1, ratio):
                 total = jnp.maximum(total, near_ref[level, g, i * ratio + c])
@@ -178,7 +212,7 @@
 
     def settle(level):
         for g in range(groups):
-            near_all(level, g).wait_send()
+            near_some(level, g, 0, side * ratio - 1).wait_send()
 
             @pl.when(jnp.logical_not(keeper))
             def _():
@@ -212,42 +246,37 @@
             peak_copy(n).start()
 
     def one_level(level, carry):
+        def one_group(g, carry):
+            compute(level, g)
+            return carry
+
+        lax.fori_loop(0, groups, one_group, 0)
+
+        @pl.when(level == last)
+        def _():
+            peaks()
+
+        @pl.when(level < last)
+        def _():
+            for k in range(side):
+                load(level + 1, k).wait()
+                widen(level + 1, k)
+
+        combine(level, groups - 3)
+        finish(level, 0)
+        combine(level, groups - 2)
+
         @pl.when(level > 0)
         def _():
-            finish(level - 1, 2)
-
-        def late():
-            @pl.when(level > 0)
-            def _():
-                finish(level - 1, 3)
-
-        compute(level, 0, [(2, late)])
-        compute(level, 1, [])
-        compute(level, 2, [(3, lambda: combine(level, 0))])
-        compute(level, 3, [(3, lambda: combine(level, 1))])
-
-        @pl.when(level == last)
-        def _():
-            peaks()
-
-        @pl.when(level < last)
-        def _():
-            load(level + 1).wait()
-            widen(level + 1)
-
-        combine(level, 2)
-
-        @pl.when(level > 0)
-        def _():
             settle(level - 1)
 
-        combine(level, 3)
-        finish(level, 0)
         finish(level, 1)
         return carry
 
     lax.fori_loop(0, level_count, one_level, 0)
-    finish(last, 2)
+    combine(last, groups - 1)
+    for g in range(2, groups - 2):
+        finish(last, g)
     top = peak_ref[0]
     for n in range(1, cols):
         peak_copy(n).wait_recv()
@@ -255,17 +284,22 @@
     top_ref[0] = top
     for n in range(1, rows):
         top_copy(n).start()
-    finish(last, 3)
+    for g in range(groups - 2, groups):
+        finish(last, g)
+
+    def give(g, k):
+        return pltpu.make_async_copy(times_ref.at[level_count, g, k], out_hbm.at[g, :, pl.ds(k * sp, sp)], out_sem)
 
     for g in range(groups):
         for k in range(side):
             wait_times(last, g, k)
-            out_ref[g * gscen:(g + 1) * gscen, k * sp:(k + 1) * sp] = times_ref[level_count, g, k]
+            give(g, k).start()
     for n in range(1, rows):
         top_copy(n).wait_recv()
         top = jnp.maximum(top, top_ref[n])
     worst_ref[...] = top
     settle(last)
+    pltpu.make_async_copy(arrival_hbm, out_hbm, out_sem).wait()
     for n in range(1, cols):
         peak_copy(n).wait_send()
     for n in range(1, rows):
@@ -280,18 +314,20 @@
     sp = tile // side
     gscen = scenarios // GROUPS
     vmem = pl.BlockSpec(memory_space=pltpu.VMEM)
+    hbm = pl.BlockSpec(memory_space=pltpu.HBM)
     f32 = jnp.float32
     dma = pltpu.SemaphoreType.DMA
     lg = (level_count, GROUPS)
     times, worst = pl.pallas_call(
         functools.partial(kernel, rows, cols),
         out_shape=(
-            jax.ShapeDtypeStruct((scenarios, tile), f32),
+            jax.ShapeDtypeStruct((GROUPS, gscen, tile), f32),
             jax.ShapeDtypeStruct((1, LANES), f32),
         ),
-        in_specs=[vmem, pl.BlockSpec(memory_space=pltpu.HBM), pl.BlockSpec(memory_space=pltpu.SMEM)],
-        out_specs=(vmem, vmem),
+        in_specs=[hbm, hbm, hbm],
+        out_specs=(hbm, vmem),
         scratch_shapes=[
+            pltpu.SMEM(occupancy.shape, occupancy.dtype),
             pltpu.VMEM((level_count, tile, width), delay.dtype),
             pltpu.VMEM((level_count, tile // 8, 8, width), f32),
             pltpu.VMEM((level_count + 1, GROUPS, side, gscen, sp), f32),
@@ -303,16 +339,16 @@
             pltpu.VMEM((GROUPS, gscen, LANES), f32),
             pltpu.VMEM((cols, 1, LANES), f32),
             pltpu.VMEM((rows, 1, LANES), f32),
-            dma((level_count,)),
-            dma(lg), dma(lg),
+            dma((side,)), dma, dma((level_count, side)), dma,
+            dma(lg), dma((*lg, side)),
             dma(lg), dma(lg),
             dma(lg), dma((*lg, side)),
             dma((cols,)), dma((cols,)),
             dma((rows,)), dma((rows,)),
         ],
         compiler_params=pltpu.CompilerParams(collective_id=0, has_side_effects=True, vmem_limit_bytes=60 * 1024 * 1024),
-    )(arrival, delay, occupancy)
-    return times, worst[0, :scenarios]
+    )(arrival.reshape(GROUPS, gscen, tile), delay, occupancy)
+    return times.reshape(scenarios, tile), worst[0, :scenarios]
 
 
 def solution(mesh):

time: 109 us -> 104 us (0.954)
  Pallas kernels: 106 us -> 101 us
    pallas_call x1, Pallas kernels: 106 us -> 101 us  [shards(): pl.pallas_call(functools.partial(kernel, rows, cols), out_shape=(jax.Shap...]
where the time goes in v2:
time: 104 us
  Pallas kernels  101 us (97%)
  local copies, waits for them, and re-layouts  2.74 us (3%)
    pallas_call x1, Pallas kernels, shards(): pl.pallas_call(functools.partial(kernel, rows, cols), out_shape=(jax.Shap...  101 us

profile of v2, /device:TPU:1, one launch (start us, length us, event | category | flops | bytes accessed | tf_op | source)
XLA Modules:
  0.0 104.1 jit_solution(6466805969528774552)
XLA Ops:
  0.6 100.7 %shard_map.50 = (f32[8,8,512]{2,1,0:T(8,128)}, f32[1,128]{1,0:T(1,128)}) custom-call(f32[8,8,512]{2,1,0:T(8,128)} %bitcast.4, bf16[4,512,1024]{2,1,0:T(8,128)(2,1)} %delay_hbm.1, s32[4,32,32]{2,1,0:T(8,128)} %occ_hbm.1), custom_call_target="tpu_custom_call" | custom-call | tf_op jit(solution)/shard_map/pallas_call | solution.py:321
  101.3 1.2 %slice_bitcast_fusion = f32[64]{0:T(128)} fusion(f32[1,128]{1,0:T(1,128)} %get-tuple-element.5), kind=kLoop, calls=%fused_computation | loop fusion | bytes 512 | tf_op jit(solution)/shard_map/squeeze | solution.py:351
  102.5 1.6 %copy.6 = f32[64,512]{1,0:T(8,128)} copy(f32[64,512]{1,0:T(8,128)} %bitcast.5) | data formatting | bytes 262144

commit v3 on v2

--- a/solution.py
+++ b/solution.py
@@ -10,6 +10,8 @@
 MESH = pl.DeviceIdType.MESH
 LANES = 128
 GROUPS = 8
+PAIR = 2
+HELD = 1
 LOW = -1000000000.0
 
 
@@ -38,13 +40,6 @@
     def greet(to_row, to_col):
         pl.semaphore_signal(barrier, inc=1, device_id=(to_row, to_col), device_id_type=MESH)
 
-    for n in range(1, cols):
-        greet(row, turn(col, n, cols))
-    for n in range(1, rows):
-        greet(turn(row, n, rows), col)
-    for i in range(1, side):
-        for c in range(1, ratio):
-            greet(turn(x, i, side) * side + y, z * ratio + turn(p, c, ratio))
     peers = cols - 1 + rows - 1 + (side - 1) * (ratio - 1)
 
     def load(level, k):
@@ -72,11 +67,18 @@
     for level in range(1, level_count):
         for k in range(side):
             load(level, k).start()
-    for k in range(side):
-        load(0, k).wait()
-        widen(0, k)
-    for k in range(side):
-        arrive(k).wait()
+    half = rows // 2
+    for n in range(half):
+        for turned in {half + n, half - n} - {0}:
+            for c in range(ratio):
+                greet(row, turn(z, turned, rows) * ratio + turn(p, c, ratio))
+    for c in range(1, ratio):
+        greet(row, z * ratio + turn(p, c, ratio))
+    for n in range(1, rows):
+        greet(turn(row, n, rows), col)
+    for i in range(1, side):
+        for c in range(1, ratio):
+            greet(turn(x, i, side) * side + y, z * ratio + turn(p, c, ratio))
     flags.wait()
 
     def near_copy(level, g, i, c):
@@ -129,58 +131,83 @@
         def _():
             times_copy(level, g, 0, 1, k).wait_recv()
 
-    def compute(level, g):
-        def step(n, best):
-            @pl.when(jnp.logical_and(jnp.logical_and(level == 0, g == 0), n == side - 1))
-            def _():
-                pl.semaphore_wait(barrier, peers)
-
-            @pl.when(n == 0)
-            def _():
-                @pl.when(jnp.logical_and(level > 0, g == 0))
-                def _():
-                    combine(level - 1, groups - 1)
-
-                @pl.when(jnp.logical_and(level > 0, g < 3))
-                def _():
-                    finish(level - 1, g + 2)
-
-            @pl.when(n == side - 1)
-            def _():
-                @pl.when(jnp.logical_and(level > 0, jnp.logical_and(g >= 2, g <= 4)))
-                def _():
-                    finish(level - 1, g + 3)
-
-                @pl.when(g >= 3)
-                def _():
-                    combine(level, g - 3)
-
-            k = turn(x, jnp.where(n < 2, n, side + 1 - n), side)
-
-            @pl.when(level > 0)
-            def _():
-                wait_times(level - 1, g, k)
-
-            value = times_ref[level, g, k]
-            for i in range(sp):
-                spread = jnp.broadcast_to(value[:, i:i + 1], (gscen, LANES))
-                best = tuple(jnp.maximum(b, spread + wide_ref[level, k * (sp // 8) + i // 8, i % 8:i % 8 + 1, c * LANES:(c + 1) * LANES]) for c, b in enumerate(best))
-            return best
-
-        best = lax.fori_loop(0, side, step, (jnp.full((gscen, LANES), LOW, jnp.float32),) * (width // LANES))
-        crest = jnp.full((gscen, LANES), LOW, jnp.float32)
-        for q in range(ratio):
-            flag = occ_ref[level, col, row * ratio + q]
-            for k in range(side):
-                piece = jnp.where(flag > 0, best[q * side + k], jnp.float32(LOW))
-                part_ref[level, g, q * side + k] = piece
-                crest = jnp.maximum(crest, piece)
-        crest_ref[g] = crest
-
+    def scatter(level, g):
         for i in (2, 1, 3, 0):
             for c in range(ratio):
                 if i or c:
                     near_copy(level, g, i, c).start()
+
+    def blank(high):
+        return (jnp.full((high, LANES), LOW, jnp.float32),) * (width // LANES)
+
+    def sweep(level, k, value, best):
+        for i in range(sp):
+            spread = jnp.broadcast_to(value[:, i:i + 1], (value.shape[0], LANES))
+            best = tuple(jnp.maximum(b, spread + wide_ref[level, k * (sp // 8) + i // 8, i % 8:i % 8 + 1, c * LANES:(c + 1) * LANES]) for c, b in enumerate(best))
+        return best
+
+    def shown(level, best):
+        flag = [occ_ref[level, col, row * ratio + q] for q in range(ratio)]
+        return [jnp.where(flag[n // side] > 0, b, jnp.float32(LOW)) for n, b in enumerate(best)]
+
+    def begin(h, carry):
+        def step(k, best):
+            @pl.when(jnp.logical_and(h == HELD, k == side - 1))
+            def _():
+                pl.semaphore_wait(barrier, peers)
+
+            @pl.when(h == 0)
+            def _():
+                load(0, k).wait()
+                arrive(k).wait()
+                widen(0, k)
+
+            @pl.when(h == groups // PAIR - 1)
+            def _():
+                @pl.when(k == 0)
+                def _():
+                    for g in range(PAIR):
+                        combine(0, g)
+
+                @pl.when(k == side - 1)
+                def _():
+                    for g in range(PAIR):
+                        combine(0, PAIR + g)
+
+            value = times_ref[0, pl.ds(h * PAIR, PAIR), k].reshape(PAIR * gscen, sp)
+            return sweep(0, k, value, best)
+
+        pieces = shown(0, lax.fori_loop(0, side, step, blank(PAIR * gscen)))
+        for n, piece in enumerate(pieces):
+            for j in range(PAIR):
+                part_ref[0, h * PAIR + j, n] = piece[j * gscen:(j + 1) * gscen]
+
+        def send(g, carry):
+            scatter(0, g)
+            return carry
+
+        lax.fori_loop(jnp.where(h == HELD, 0, h * PAIR), jnp.where(h < HELD, h * PAIR, (h + 1) * PAIR), send, 0)
+        return carry
+
+    def compute(level, g):
+        def step(n, best):
+            @pl.when(jnp.logical_and(n == 0, g < groups - 2))
+            def _():
+                finish(level - 1, g + 2)
+
+            @pl.when(jnp.logical_and(n == side - 1, g >= 3))
+            def _():
+                combine(level, g - 3)
+
+            k = turn(x, jnp.where(n < 2, n, side + 1 - n), side)
+            wait_times(level - 1, g, k)
+            return sweep(level, k, times_ref[level, g, k], best)
+
+        pieces = shown(level, lax.fori_loop(0, side, step, blank(gscen)))
+        for n, piece in enumerate(pieces):
+            part_ref[level, g, n] = piece
+        crest_ref[g] = functools.reduce(jnp.maximum, pieces)
+        scatter(level, g)
 
     def combine(level, g):
         for i in (0, 1, 3, 2):
@@ -239,11 +266,16 @@
         peak = jnp.full((1, LANES), LOW, jnp.float32)
         for g in range(groups):
             most = jnp.max(crest_ref[g], axis=1, keepdims=True)
-            shown = jnp.where(lane == line + g * gscen, most, jnp.float32(LOW))
-            peak = jnp.maximum(peak, jnp.max(shown, axis=0, keepdims=True))
+            placed = jnp.where(lane == line + g * gscen, most, jnp.float32(LOW))
+            peak = jnp.maximum(peak, jnp.max(placed, axis=0, keepdims=True))
         peak_ref[0] = peak
         for n in range(1, cols):
             peak_copy(n).start()
+
+    def ready(level):
+        for k in range(side):
+            load(level, k).wait()
+            widen(level, k)
 
     def one_level(level, carry):
         def one_group(g, carry):
@@ -251,30 +283,29 @@
             return carry
 
         lax.fori_loop(0, groups, one_group, 0)
-
-        @pl.when(level == last)
-        def _():
-            peaks()
+        pl.when(level == last)(peaks)
+        combine(level, 5)
+        finish(level, 0)
+        combine(level, 6)
 
         @pl.when(level < last)
         def _():
-            for k in range(side):
-                load(level + 1, k).wait()
-                widen(level + 1, k)
-
-        combine(level, groups - 3)
-        finish(level, 0)
-        combine(level, groups - 2)
-
-        @pl.when(level > 0)
-        def _():
-            settle(level - 1)
+            ready(level + 1)
 
         finish(level, 1)
+        combine(level, 7)
+        settle(level - 1)
         return carry
 
-    lax.fori_loop(0, level_count, one_level, 0)
-    combine(last, groups - 1)
+    lax.fori_loop(0, groups // PAIR, begin, 0)
+    combine(0, 4)
+    combine(0, 5)
+    finish(0, 0)
+    combine(0, 6)
+    ready(1)
+    finish(0, 1)
+    combine(0, 7)
+    lax.fori_loop(1, level_count, one_level, 0)
     for g in range(2, groups - 2):
         finish(last, g)
     top = peak_ref[0]
@@ -325,7 +356,7 @@
             jax.ShapeDtypeStruct((1, LANES), f32),
         ),
         in_specs=[hbm, hbm, hbm],
-        out_specs=(hbm, vmem),
+        out_specs=(pl.BlockSpec(memory_space=pl.ANY), vmem),
         scratch_shapes=[
             pltpu.SMEM(occupancy.shape, occupancy.dtype),
             pltpu.VMEM((level_count, tile, width), delay.dtype),
@@ -346,8 +377,8 @@
             dma((cols,)), dma((cols,)),
             dma((rows,)), dma((rows,)),
         ],
-        compiler_params=pltpu.CompilerParams(collective_id=0, has_side_effects=True, vmem_limit_bytes=60 * 1024 * 1024),
-    )(arrival.reshape(GROUPS, gscen, tile), delay, occupancy)
+        compiler_params=pltpu.CompilerParams(collective_id=0, has_side_effects=True, vmem_limit_bytes=40 * 1024 * 1024),
+    )(*(pltpu.with_memory_space_constraint(v, pltpu.HBM) for v in (arrival.reshape(GROUPS, gscen, tile), delay, occupancy)))
     return times.reshape(scenarios, tile), worst[0, :scenarios]
 
 

time: 104 us -> 99.8 us (0.960)
  Pallas kernels: 101 us -> 97.9 us
  local copies, waits for them, and re-layouts: 2.74 us -> 1.17 us
    pallas_call x1, Pallas kernels: 101 us -> 97.9 us  [shards(): pl.pallas_call(functools.partial(kernel, rows, cols), out_shape=(jax.Shap...]
where the time goes in v3:
time: 99.8 us; the launch traced here: 99.7 us
  Pallas kernels  97.9 us (98%)
  local copies, waits for them, and re-layouts  1.17 us (1%)
    pallas_call x1, Pallas kernels, shards(): pl.pallas_call(functools.partial(kernel, rows, cols), out_shape=(jax.Shap...  97.9 us

profile of v3, /device:TPU:1, one launch (start us, length us, event | category | flops | bytes accessed | tf_op | source)
XLA Modules:
  0.0 99.7 jit_solution(12544274407200166712)
XLA Ops:
  0.6 97.9 %shard_map.50 = (f32[8,8,512]{2,1,0:T(8,128)S(1)}, f32[1,128]{1,0:T(1,128)S(1)}) custom-call(f32[8,8,512]{2,1,0:T(8,128)} %bitcast.5, bf16[4,512,1024]{2,1,0:T(8,128)(2,1)} %delay_hbm.1, s32[4,32,32]{2,1,0:T(8,128)} %occ_hbm.1), custom_call_target="tpu_custom_call" | custom-call | tf_op jit(solution)/shard_map/pallas_call | solution.py:352
  98.5 0.5 slice_bitcast_fusion
  99.0 0.7 copy.6

commit v4 on v3

--- a/solution.py
+++ b/solution.py
@@ -127,9 +127,7 @@
             device_id=(turn(row, 1, rows), col), device_id_type=MESH)
 
     def wait_times(level, g, k):
-        @pl.when(jnp.logical_not(jnp.logical_and(keeper, k == x)))
-        def _():
-            times_copy(level, g, 0, 1, k).wait_recv()
+        times_copy(level, g, 0, 1, k).wait_recv()
 
     def scatter(level, g):
         for i in (2, 1, 3, 0):
@@ -195,15 +193,17 @@
             def _():
                 finish(level - 1, g + 2)
 
-            @pl.when(jnp.logical_and(n == side - 1, g >= 3))
+            @pl.when(jnp.logical_and(n == 1, g >= 3))
             def _():
                 combine(level, g - 3)
 
-            k = turn(x, jnp.where(n < 2, n, side + 1 - n), side)
-            wait_times(level - 1, g, k)
-            return sweep(level, k, times_ref[level, g, k], best)
-
-        pieces = shown(level, lax.fori_loop(0, side, step, blank(gscen)))
+            for off in ((side - 1) * n, 1 + n):
+                k = turn(x, off, side)
+                wait_times(level - 1, g, k)
+                best = sweep(level, k, times_ref[level, g, k], best)
+            return best
+
+        pieces = shown(level, lax.fori_loop(0, side // 2, step, blank(gscen)))
         for n, piece in enumerate(pieces):
             part_ref[level, g, n] = piece
         crest_ref[g] = functools.reduce(jnp.maximum, pieces)
@@ -235,7 +235,7 @@
             fin_ref[level, g] = total
             for a, b in steps:
                 times_copy(level, g, a, b, x).start()
-            times_ref[level + 1, g, x] = total
+            pltpu.make_async_copy(fin_ref.at[level, g], times_ref.at[level + 1, g, x], times_recv.at[level, g, x]).start()
 
     def settle(level):
         for g in range(groups):

time: 99.8 us -> 98.4 us (0.986)
  Pallas kernels: 97.9 us -> 96.5 us
    pallas_call x1, Pallas kernels: 97.9 us -> 96.5 us  [shards(): pl.pallas_call(functools.partial(kernel, rows, cols), out_shape=(jax.Shap...]
where the time goes in v4:
time: 98.4 us; the launch traced here: 98.3 us
  Pallas kernels  96.5 us (98%)
  local copies, waits for them, and re-layouts  1.17 us (1%)
    pallas_call x1, Pallas kernels, shards(): pl.pallas_call(functools.partial(kernel, rows, cols), out_shape=(jax.Shap...  96.5 us

profile of v4, /device:TPU:1, one launch (start us, length us, event | category | flops | bytes accessed | tf_op | source)
XLA Modules:
  0.0 98.3 jit_solution(12773606526231658062)
XLA Ops:
  0.6 96.5 %shard_map.50 = (f32[8,8,512]{2,1,0:T(8,128)S(1)}, f32[1,128]{1,0:T(1,128)S(1)}) custom-call(f32[8,8,512]{2,1,0:T(8,128)} %bitcast.5, bf16[4,512,1024]{2,1,0:T(8,128)(2,1)} %delay_hbm.1, s32[4,32,32]{2,1,0:T(8,128)} %occ_hbm.1), custom_call_target="tpu_custom_call" | custom-call | tf_op jit(solution)/shard_map/pallas_call | solution.py:352
  97.1 0.5 slice_bitcast_fusion
  97.6 0.7 copy.6
